TPU v7x, 32 devices: a whole 2x2x4 slice. The times are simulated.
32 devices in a mesh: seq: 8 (over z, y), chan: 4 (over x, core).
Axes of the slice: x: 2, y: 2, z: 4, core: 2. Of those that a mesh axis runs over, the one named last changes fastest.
Arguments:
- inputs: float32 [1024, 8192], P('seq', 'chan'), may hold values from -6 to 6
- conv_weight: float32 [3, 4, 8192], P(None, None, 'chan'), may hold values from -3 to 3
- conv_bias: float32 [3, 8192], P(None, 'chan'), may hold values from -1 to 1
- cotangent: float32 [1024, 8192], P('seq', 'chan'), may hold values from -6 to 6
Outputs:
- output: float32 [1024, 8192], P('seq', 'chan')
- input_grad: float32 [1024, 8192], P('seq', 'chan')
- weight_grad: float32 [3, 4, 8192], P(None, None, 'chan')
- bias_grad: float32 [3, 8192], P(None, 'chan')
All inputs are finite; a program needn't handle non-finite values.
Results may differ from a plain program's by a relative error of at most 0.0001.
Values sent between devices are 32-bit elements; how exact they have to be, the bound alone decides.
No kernel may reach another device: no remote copies, remote signals or barrier semaphores. Data moves between devices by JAX's collectives and lax.ppermute only.
A program may use at most 64 MiB of HBM per device.

v0:
```python
import jax
import jax.numpy as jnp
from jax import lax
from jax.sharding import PartitionSpec as P


def passed_along(array, axis, by):
    devices = lax.axis_size(axis)
    pairs = [(i, i + by) for i in range(devices) if 0 <= i + by < devices]
    return lax.ppermute(array, axis, pairs)


def shards(inputs, conv_weight, conv_bias, cotangent):
    shard_len = inputs.shape[0]
    layers = conv_weight.shape[0]
    taps = conv_weight.shape[1]
    act = inputs
    saved = []
    for layer in range(layers):
        before = passed_along(act[shard_len - (taps - 1) :], "seq", 1)
        padded = jnp.concatenate([before, act], axis=0)
        preact = conv_bias[layer][None, :] + sum(
            (
                conv_weight[layer, offset][None, :] * padded[offset : offset + shard_len]
                for offset in range(taps)
            )
        )
        saved.append((padded, preact))
        act = preact * jax.nn.sigmoid(preact)
    grad = cotangent
    term_list = [None] * layers
    for layer in reversed(range(layers)):
        padded, preact = saved[layer]
        gate_value = jax.nn.sigmoid(preact)
        pre_grad = grad * gate_value * (1.0 + preact * (1.0 - gate_value))
        after = passed_along(pre_grad[: taps - 1], "seq", -1)
        grad_pad = jnp.concatenate([pre_grad, after], axis=0)
        grad = sum(
            (
                conv_weight[layer, offset][None, :]
                * grad_pad[taps - 1 - offset : taps - 1 - offset + shard_len]
                for offset in range(taps)
            )
        )
        weight_terms = [
            jnp.sum(pre_grad * padded[offset : offset + shard_len], axis=0)
            for offset in range(taps)
        ]
        term_list[layer] = jnp.stack(weight_terms + [jnp.sum(pre_grad, axis=0)])
    all_terms = jnp.stack(term_list)
    summed = lax.psum(all_terms, "seq")
    return (act, grad, summed[:, :taps], summed[:, taps])


def solution(mesh):
    in_specs = (P("seq", "chan"), P(None, None, "chan"), P(None, "chan"), P("seq", "chan"))
    out_specs = (P("seq", "chan"), P("seq", "chan"), P(None, None, "chan"), P(None, "chan"))
    return jax.shard_map(shards, mesh=mesh, in_specs=in_specs, out_specs=out_specs, check_vma=False)
```

profile of v0, /device:TPU:0, one launch (start us, length us, event | category | flops | bytes accessed | tf_op | source)
XLA Modules:
  0.0 137.0 jit_solution(2371675134209580371)
XLA Ops:
  7.2 0.0 all-reduce.2.cloned.1.call-start
  7.2 0.9 slice.150
  8.1 4.9 %collective-permute-start = (f32[3,2048]{1,0:T(4,128)S(1)}, f32[3,2048]{1,0:T(4,128)S(1)}, u32[]{:S(2)}, u32[]{:S(2)}) collective-permute-start(f32[3,2048]{1,0:T(4,128)S(1)} %slice.150), channel_id=1, source_target_pairs={{0,4},{4,8},{8,12},{12,16},{16,20},{20,24},{24,28},{1,5},{5,9},{9,... | collective-permute-start | bytes 73736 | tf_op jit(solution)/shard_map/ppermute | solution.py:10
  13.0 1.1 fusion.41
  14.1 0.9 fusion.42
  15.0 3.4 %fusion.36 = (f32[128,2048]{1,0:T(8,128)S(1)}, f32[128,2048]{1,0:T(8,128)S(1)}) fusion(f32[128,2048]{1,0:T(8,128)} %param.4, f32[2048]{0:T(1024)S(1)} %bitcast.32, f32[3,2048]{1,0:T(4,128)S(1)} %collective-permute-done, f32[2048]{0:T(1024)S(1)} %bitcast.34, f32[2048]{0:T(1024)S(1)} %bitcast.36, f32[2048]{0:T(1024)S(1)} %bitcast.38, f32[2048]{0:T(1024)S(1)} %bitcast.58), kind=kLoop, calls=%fused_computation.84 | loop fusion | flops 3932160 | bytes 3211264 | tf_op jit(solution)/shard_map/mul | solution.py:29
  18.4 3.8 %collective-permute-start.1 = (f32[3,2048]{1,0:T(4,128)S(1)}, f32[3,2048]{1,0:T(4,128)S(1)}, u32[]{:S(2)}, u32[]{:S(2)}) collective-permute-start(f32[3,2048]{1,0:T(4,128)S(1)} %slice.189), channel_id=1, source_target_pairs={{0,4},{4,8},{8,12},{12,16},{16,20},{20,24},{24,28},{1,5},{5,9},{9,... | collective-permute-start | bytes 73736 | tf_op jit(solution)/shard_map/ppermute | solution.py:10
  22.2 1.6 %collective-permute-done.1 = f32[3,2048]{1,0:T(4,128)S(1)} collective-permute-done((f32[3,2048]{1,0:T(4,128)S(1)}, f32[3,2048]{1,0:T(4,128)S(1)}, u32[]{:S(2)}, u32[]{:S(2)}) %collective-permute-start.1) | collective-permute-done | bytes 24608 | tf_op jit(solution)/shard_map/ppermute | solution.py:10
  23.8 0.7 fusion.35
  24.5 4.3 %collective-permute-start.2 = (f32[3,2048]{1,0:T(4,128)S(1)}, f32[3,2048]{1,0:T(4,128)S(1)}, u32[]{:S(2)}, u32[]{:S(2)}) collective-permute-start(f32[3,2048]{1,0:T(4,128)S(1)} %slice.194), channel_id=1, source_target_pairs={{0,4},{4,8},{8,12},{12,16},{16,20},{20,24},{24,28},{1,5},{5,9},{9,... | collective-permute-start | bytes 73736 | tf_op jit(solution)/shard_map/ppermute | solution.py:10
  28.8 1.6 %collective-permute-done.2 = f32[3,2048]{1,0:T(4,128)S(1)} collective-permute-done((f32[3,2048]{1,0:T(4,128)S(1)}, f32[3,2048]{1,0:T(4,128)S(1)}, u32[]{:S(2)}, u32[]{:S(2)}) %collective-permute-start.2) | collective-permute-done | bytes 24608 | tf_op jit(solution)/shard_map/ppermute | solution.py:10
  30.4 1.5 %fusion.38 = (f32[2048]{0:T(1024)S(1)}, f32[2048]{0:T(1024)S(1)}, f32[2048]{0:T(1024)S(1)}, f32[2048]{0:T(1024)S(1)}, f32[2048]{0:T(1024)S(1)}, /*index=5*/f32[128,2048]{1,0:T(8,128)S(1)}, f32[128,2048]{1,0:T(8,128)S(1)}) fusion(f32[128,2048]{1,0:T(8,128)S(1)} %get-tuple-element.34, f32[128,2048]{1,0:T(8,128)S(1)} %get-tuple-element.33, ...), kind=kLoop, calls=%fused_computation.89 | loop fusion | flops 8902656 | bytes 5349376 | tf_op jit(solution)/shard_map/reduce_sum | solution.py:49
  31.9 1.3 collective-permute-start.3
  33.2 5.7 %collective-permute-done.3 = f32[3,2048]{1,0:T(4,128)S(1)} collective-permute-done((f32[3,2048]{1,0:T(4,128)S(1)}, f32[3,2048]{1,0:T(4,128)S(1)}, u32[]{:S(2)}, u32[]{:S(2)}) %collective-permute-start.3) | collective-permute-done | bytes 24608 | tf_op jit(solution)/shard_map/ppermute | solution.py:10
  38.9 1.7 %fusion.37 = (f32[2048]{0:T(1024)S(1)}, f32[2048]{0:T(1024)S(1)}, f32[2048]{0:T(1024)S(1)}, f32[2048]{0:T(1024)S(1)}, f32[2048]{0:T(1024)S(1)}, /*index=5*/f32[128,2048]{1,0:T(8,128)S(1)}) fusion(f32[128,2048]{1,0:T(8,128)S(1)} %get-tuple-element.36, f32[128,2048]{1,0:T(8,128)S(1)} %get-tuple-element.35, f32[3,2048]{1,0:T(4,128)S(1)} %collective-permute-done.1, ...), kind=kLoop, calls=%fused_computation.88 | loop fusion | flops 8902656 | bytes 5365760 | tf_op jit(solution)/shard_map/reduce_sum | solution.py:49
  40.6 0.0 copy-start.1
  40.6 1.3 collective-permute-start.4
  41.9 1.3 fusion.34
  43.2 0.1 stack.85
  43.3 0.1 stack.78
  43.4 4.2 %collective-permute-done.4 = f32[3,2048]{1,0:T(4,128)S(1)} collective-permute-done((f32[3,2048]{1,0:T(4,128)S(1)}, f32[3,2048]{1,0:T(4,128)S(1)}, u32[]{:S(2)}, u32[]{:S(2)}) %collective-permute-start.4) | collective-permute-done | bytes 24608 | tf_op jit(solution)/shard_map/ppermute | solution.py:10
  47.7 3.3 %multiply_reduce_fusion.9 = (f32[2048]{0:T(1024)S(1)}, f32[2048]{0:T(1024)S(1)}, f32[2048]{0:T(1024)S(1)}, f32[2048]{0:T(1024)S(1)}, f32[2048]{0:T(1024)S(1)}, /*index=5*/f32[128,2048]{1,0:T(8,128)S(1)}) fusion(f32[128,2048]{1,0:T(8,128)S(1)} %copy-done, f32[3,2048]{1,0:T(4,128)S(1)} %collective-permute-done, f32[128,2048]{1,0:T(8,128)S(1)} %get-tuple-element.36, ...), kind=kLoop, calls=%fused_computation.73 | loop fusion | flops 7854080 | bytes 4317184 | tf_op jit(solution)/shard_map/reduce_sum | solution.py:46
  51.0 0.1 stack.71
  51.1 1.3 collective-permute-start.5
  52.4 0.8 pad_maximum_fusion.6
  53.2 0.0 all-reduce.2.cloned.1.call-update
  53.2 4.6 %collective-permute-done.5 = f32[3,2048]{1,0:T(4,128)S(1)} collective-permute-done((f32[3,2048]{1,0:T(4,128)S(1)}, f32[3,2048]{1,0:T(4,128)S(1)}, u32[]{:S(2)}, u32[]{:S(2)}) %collective-permute-start.5) | collective-permute-done | bytes 24608 | tf_op jit(solution)/shard_map/ppermute | solution.py:10
  57.8 1.4 %fusion.4 = f32[128,2048]{1,0:T(8,128)} fusion(f32[128,2048]{1,0:T(8,128)S(1)} %get-tuple-element.29, f32[3,2048]{1,0:T(4,128)S(1)} %collective-permute-done.5, f32[2048]{0:T(1024)S(1)} %bitcast.33, f32[2048]{0:T(1024)S(1)} %bitcast.35, f32[2048]{0:T(1024)S(1)} %bitcast.37, f32[2048]{0:T(1024)S(1)} %bitcast.39), kind=kLoop, calls=%fused_computation.28 | loop fusion | flops 2621440 | bytes 2154496 | tf_op jit(solution)/shard_map/add | solution.py:38
  59.3 67.9 %all-reduce.2.cloned.1.call-done = f32[3,5,2048]{2,0,1:T(4,128)} async-done(((f32[3,5,2048]{2,0,1:T(4,128)}), f32[3,5,2048]{2,0,1:T(4,128)}) %all-reduce.2.cloned.1.call-update) | async-done | bytes 122896 | tf_op jit(solution)/shard_map/psum | solution.py:51
  127.1 0.9 slice.214
  128.1 0.7 copy.8
  128.8 1.4 %slice_bitcast_fusion = f32[3,2048]{1,0:T(4,128)} fusion(f32[3,5,2048]{2,0,1:T(4,128)} %all-reduce.2.cloned.1.call-done), kind=kLoop, calls=%fused_computation.87 | loop fusion | bytes 49152 | tf_op jit(solution)/shard_map/squeeze | solution.py:52
  (14 shorter events, 0.1 us)
Async XLA Ops:
  7.2 120.0 %all-reduce.2.cloned.1.call-start = ((), (), s32[]{:S(2)}) async-start(), calls=%async_computation | async-start | bytes 327680 | tf_op jit(solution)/shard_map/psum | solution.py:51
  8.1 6.9 %collective-permute-start = (f32[3,2048]{1,0:T(4,128)S(1)}, f32[3,2048]{1,0:T(4,128)S(1)}, u32[]{:S(2)}, u32[]{:S(2)}) collective-permute-start(f32[3,2048]{1,0:T(4,128)S(1)} %slice.150), channel_id=1, source_target_pairs={{0,4},{4,8},{8,12},{12,16},{16,20},{20,24},{24,28},{1,5},{5,9},{9,... | collective-permute-start | bytes 73736 | tf_op jit(solution)/shard_map/ppermute | solution.py:10
  18.4 5.4 %collective-permute-start.1 = (f32[3,2048]{1,0:T(4,128)S(1)}, f32[3,2048]{1,0:T(4,128)S(1)}, u32[]{:S(2)}, u32[]{:S(2)}) collective-permute-start(f32[3,2048]{1,0:T(4,128)S(1)} %slice.189), channel_id=1, source_target_pairs={{0,4},{4,8},{8,12},{12,16},{16,20},{20,24},{24,28},{1,5},{5,9},{9,... | collective-permute-start | bytes 73736 | tf_op jit(solution)/shard_map/ppermute | solution.py:10
  23.8 6.6 %copy-start.2 = (f32[128,2048]{1,0:T(8,128)S(1)}, f32[128,2048]{1,0:T(8,128)}, u32[]{:S(2)}) copy-start(f32[128,2048]{1,0:T(8,128)} %param.7) | copy-start | bytes 3145732
  24.5 5.9 %collective-permute-start.2 = (f32[3,2048]{1,0:T(4,128)S(1)}, f32[3,2048]{1,0:T(4,128)S(1)}, u32[]{:S(2)}, u32[]{:S(2)}) collective-permute-start(f32[3,2048]{1,0:T(4,128)S(1)} %slice.194), channel_id=1, source_target_pairs={{0,4},{4,8},{8,12},{12,16},{16,20},{20,24},{24,28},{1,5},{5,9},{9,... | collective-permute-start | bytes 73736 | tf_op jit(solution)/shard_map/ppermute | solution.py:10
  31.9 7.0 %collective-permute-start.3 = (f32[3,2048]{1,0:T(4,128)S(1)}, f32[3,2048]{1,0:T(4,128)S(1)}, u32[]{:S(2)}, u32[]{:S(2)}) collective-permute-start(f32[3,2048]{1,0:T(4,128)S(1)} %slice.199), channel_id=1, source_target_pairs={{4,0},{8,4},{12,8},{16,12},{20,16},{24,20},{28,24},{5,1},{9,5},{13... | collective-permute-start | bytes 73736 | tf_op jit(solution)/shard_map/ppermute | solution.py:10
  40.6 2.6 %copy-start.1 = (f32[128,2048]{1,0:T(8,128)}, f32[128,2048]{1,0:T(8,128)S(1)}, u32[]{:S(2)}) copy-start(f32[128,2048]{1,0:T(8,128)S(1)} %get-tuple-element.30) | copy-start | bytes 3145732
  40.6 7.0 %collective-permute-start.4 = (f32[3,2048]{1,0:T(4,128)S(1)}, f32[3,2048]{1,0:T(4,128)S(1)}, u32[]{:S(2)}, u32[]{:S(2)}) collective-permute-start(f32[3,2048]{1,0:T(4,128)S(1)} %slice.204), channel_id=1, source_target_pairs={{4,0},{8,4},{12,8},{16,12},{20,16},{24,20},{28,24},{5,1},{9,5},{13... | collective-permute-start | bytes 73736 | tf_op jit(solution)/shard_map/ppermute | solution.py:10
  41.9 5.7 %copy-start = (f32[128,2048]{1,0:T(8,128)S(1)}, f32[128,2048]{1,0:T(8,128)}, u32[]{:S(2)}) copy-start(f32[128,2048]{1,0:T(8,128)} %param.4) | copy-start | bytes 3145732
  51.1 6.7 %collective-permute-start.5 = (f32[3,2048]{1,0:T(4,128)S(1)}, f32[3,2048]{1,0:T(4,128)S(1)}, u32[]{:S(2)}, u32[]{:S(2)}) collective-permute-start(f32[3,2048]{1,0:T(4,128)S(1)} %slice.209), channel_id=1, source_target_pairs={{4,0},{8,4},{12,8},{16,12},{20,16},{24,20},{28,24},{5,1},{9,5},{13... | collective-permute-start | bytes 73736 | tf_op jit(solution)/shard_map/ppermute | solution.py:10
Sparse Core Ops, SparseCore 0:
  53.3 73.7 all-reduce.1
where the time goes:
time: 138 us; the launch traced here: 137 us
  waiting for transfers between devices  85.6 us (62%)
  starting transfers between devices  16.9 us (12%)
  between operations  14.2 us (10%)
  other arithmetic  14.1 us (10%)
  local copies, waits for them, and re-layouts  6.21 us (4%)
    psum x1, waiting for transfers between devices, shards(): summed = lax.psum(all_terms, 'seq')  67.9 us
    ppermute x6, waiting for transfers between devices, passed_along(): return lax.ppermute(array, axis, pairs)  17.7 us
    ppermute x6, starting transfers between devices, passed_along(): return lax.ppermute(array, axis, pairs)  16.9 us
    mul x3, other arithmetic, shards(): act = preact * jax.nn.sigmoid(preact)  5.36 us
    reduce_sum x1, other arithmetic, shards(): jnp.sum(pre_grad * padded[offset:offset + shard_len], axis=0)  3.34 us
    reduce_sum x2, other arithmetic, shards(): term_list[layer] = jnp.stack(weight_terms + [jnp.sum(pre_grad, axis=0)])  3.17 us
  transfers between devices with their start and end apart: 7, of which 6 were waited for; matrix products, arithmetic and copies ran while one was open for 4% of the time, Pallas kernels for 0%

commit v1 on v0

--- a/solution.py
+++ b/solution.py
@@ -48,7 +48,7 @@
         ]
         term_list[layer] = jnp.stack(weight_terms + [jnp.sum(pre_grad, axis=0)])
     all_terms = jnp.stack(term_list)
-    summed = lax.psum(all_terms, "seq")
+    summed = jnp.sum(lax.all_gather(all_terms, "seq"), axis=0)
     return (act, grad, summed[:, :taps], summed[:, taps])
 
 

time: 138 us -> 91 us (0.66)
  waiting for transfers between devices: 85.6 us -> 13.2 us
  blocking collectives: 0 us -> 40.1 us
  between operations: 14.2 us -> 0.78 us
    psum x1 -> x0, waiting for transfers between devices: 67.9 us -> none  [shards(): summed = lax.psum(all_terms, 'seq')]
    all_gather x0 -> x1, blocking collectives: none -> 40.1 us  [shards(): summed = jnp.sum(lax.all_gather(all_terms, 'seq'), axis=0)]
    ppermute x6, waiting for transfers between devices: 17.7 us -> 13.2 us  [passed_along(): return lax.ppermute(array, axis, pairs)]
  transfers between devices with their start and end apart: 7 -> 6, of which waited for: 6 -> 4; matrix products, arithmetic and copies ran while one was open for 4% -> 6% of each run, Pallas kernels for 0% -> 0%
where the time goes in v1:
time: 91 us; the launch traced here: 90.5 us
  blocking collectives  40.1 us (44%)
  starting transfers between devices  16.8 us (18%)
  other arithmetic  14.3 us (16%)
  waiting for transfers between devices  13.2 us (15%)
  local copies, waits for them, and re-layouts  5.35 us (6%)
    all_gather x1, blocking collectives, shards(): summed = jnp.sum(lax.all_gather(all_terms, 'seq'), axis=0)  40.1 us
    ppermute x6, starting transfers between devices, passed_along(): return lax.ppermute(array, axis, pairs)  16.8 us
    ppermute x6, waiting for transfers between devices, passed_along(): return lax.ppermute(array, axis, pairs)  13.2 us
    mul x3, other arithmetic, shards(): act = preact * jax.nn.sigmoid(preact)  5.06 us
    reduce_sum x2, other arithmetic, shards(): term_list[layer] = jnp.stack(weight_terms + [jnp.sum(pre_grad, axis=0)])  3.9 us
    reduce_sum x1, other arithmetic, shards(): jnp.sum(pre_grad * padded[offset:offset + shard_len], axis=0)  3.76 us
  transfers between devices with their start and end apart: 6, of which 4 were waited for; matrix products, arithmetic and copies ran while one was open for 6% of the time, Pallas kernels for 0%

profile of v1, /device:TPU:0, one launch (start us, length us, event | category | flops | bytes accessed | tf_op | source)
XLA Modules:
  0.0 90.5 jit_solution(1519769035003645062)
XLA Ops:
  0.6 0.9 slice.150
  1.5 4.9 %collective-permute-start = (f32[3,2048]{1,0:T(4,128)S(1)}, f32[3,2048]{1,0:T(4,128)S(1)}, u32[]{:S(2)}, u32[]{:S(2)}) collective-permute-start(f32[3,2048]{1,0:T(4,128)S(1)} %slice.150), channel_id=1, source_target_pairs={{0,4},{4,8},{8,12},{12,16},{16,20},{20,24},{24,28},{1,5},{5,9},{9,... | collective-permute-start | bytes 73736 | tf_op jit(solution)/shard_map/ppermute | solution.py:10
  6.4 1.2 %fusion.41 = (f32[1,1,2048]{2,1,0:T(1,128)S(1)}, f32[1,1,2048]{2,1,0:T(1,128)S(1)}, f32[1,1,2048]{2,1,0:T(1,128)S(1)}, f32[1,1,2048]{2,1,0:T(1,128)S(1)}, f32[1,...) fusion(f32[3,4,2048]{2,1,0:T(4,128)} %param.5), kind=kLoop, calls=%fused_computation.90 | loop fusion | bytes 196608 | tf_op jit(solution)/shard_map/slice | solution.py:24
  7.6 0.9 fusion.42
  8.5 0.0 collective-permute-done
  8.5 3.1 %fusion.36 = (f32[128,2048]{1,0:T(8,128)S(1)}, f32[128,2048]{1,0:T(8,128)S(1)}) fusion(f32[128,2048]{1,0:T(8,128)} %param.4, f32[2048]{0:T(1024)S(1)} %bitcast.41, f32[3,2048]{1,0:T(4,128)S(1)} %collective-permute-done, f32[2048]{0:T(1024)S(1)} %bitcast.43, f32[2048]{0:T(1024)S(1)} %bitcast.45, f32[2048]{0:T(1024)S(1)} %bitcast.47, f32[2048]{0:T(1024)S(1)} %bitcast.67), kind=kLoop, calls=%fused_computation.84 | loop fusion | flops 3932160 | bytes 3211264 | tf_op jit(solution)/shard_map/mul | solution.py:29
  11.6 3.7 %collective-permute-start.1 = (f32[3,2048]{1,0:T(4,128)S(1)}, f32[3,2048]{1,0:T(4,128)S(1)}, u32[]{:S(2)}, u32[]{:S(2)}) collective-permute-start(f32[3,2048]{1,0:T(4,128)S(1)} %slice.189), channel_id=1, source_target_pairs={{0,4},{4,8},{8,12},{12,16},{16,20},{20,24},{24,28},{1,5},{5,9},{9,... | collective-permute-start | bytes 73736 | tf_op jit(solution)/shard_map/ppermute | solution.py:10
  15.3 1.6 %collective-permute-done.1 = f32[3,2048]{1,0:T(4,128)S(1)} collective-permute-done((f32[3,2048]{1,0:T(4,128)S(1)}, f32[3,2048]{1,0:T(4,128)S(1)}, u32[]{:S(2)}, u32[]{:S(2)}) %collective-permute-start.1) | collective-permute-done | bytes 24608 | tf_op jit(solution)/shard_map/ppermute | solution.py:10
  16.9 0.7 fusion.35
  17.6 4.3 %collective-permute-start.2 = (f32[3,2048]{1,0:T(4,128)S(1)}, f32[3,2048]{1,0:T(4,128)S(1)}, u32[]{:S(2)}, u32[]{:S(2)}) collective-permute-start(f32[3,2048]{1,0:T(4,128)S(1)} %slice.194), channel_id=1, source_target_pairs={{0,4},{4,8},{8,12},{12,16},{16,20},{20,24},{24,28},{1,5},{5,9},{9,... | collective-permute-start | bytes 73736 | tf_op jit(solution)/shard_map/ppermute | solution.py:10
  21.9 1.6 %collective-permute-done.2 = f32[3,2048]{1,0:T(4,128)S(1)} collective-permute-done((f32[3,2048]{1,0:T(4,128)S(1)}, f32[3,2048]{1,0:T(4,128)S(1)}, u32[]{:S(2)}, u32[]{:S(2)}) %collective-permute-start.2) | collective-permute-done | bytes 24608 | tf_op jit(solution)/shard_map/ppermute | solution.py:10
  23.5 0.0 copy-done.1
  23.5 1.5 %fusion.38 = (f32[2048]{0:T(1024)S(1)}, f32[2048]{0:T(1024)S(1)}, f32[2048]{0:T(1024)S(1)}, f32[2048]{0:T(1024)S(1)}, f32[2048]{0:T(1024)S(1)}, /*index=5*/f32[128,2048]{1,0:T(8,128)S(1)}, f32[128,2048]{1,0:T(8,128)S(1)}) fusion(f32[128,2048]{1,0:T(8,128)S(1)} %get-tuple-element.38, f32[128,2048]{1,0:T(8,128)S(1)} %get-tuple-element.37, ...), kind=kLoop, calls=%fused_computation.89 | loop fusion | flops 8902656 | bytes 5349376 | tf_op jit(solution)/shard_map/reduce_sum | solution.py:49
  25.0 1.3 %collective-permute-start.3 = (f32[3,2048]{1,0:T(4,128)S(1)}, f32[3,2048]{1,0:T(4,128)S(1)}, u32[]{:S(2)}, u32[]{:S(2)}) collective-permute-start(f32[3,2048]{1,0:T(4,128)S(1)} %slice.199), channel_id=1, source_target_pairs={{4,0},{8,4},{12,8},{16,12},{20,16},{24,20},{28,24},{5,1},{9,5},{13... | collective-permute-start | bytes 73736 | tf_op jit(solution)/shard_map/ppermute | solution.py:10
  26.3 5.7 %collective-permute-done.3 = f32[3,2048]{1,0:T(4,128)S(1)} collective-permute-done((f32[3,2048]{1,0:T(4,128)S(1)}, f32[3,2048]{1,0:T(4,128)S(1)}, u32[]{:S(2)}, u32[]{:S(2)}) %collective-permute-start.3) | collective-permute-done | bytes 24608 | tf_op jit(solution)/shard_map/ppermute | solution.py:10
  32.0 2.4 %fusion.37 = (f32[2048]{0:T(1024)S(1)}, f32[2048]{0:T(1024)S(1)}, f32[2048]{0:T(1024)S(1)}, f32[2048]{0:T(1024)S(1)}, f32[2048]{0:T(1024)S(1)}, /*index=5*/f32[128,2048]{1,0:T(8,128)}) fusion(f32[128,2048]{1,0:T(8,128)S(1)} %get-tuple-element.40, f32[128,2048]{1,0:T(8,128)S(1)} %get-tuple-element.39, f32[3,2048]{1,0:T(4,128)S(1)} %collective-permute-done.1, ...), kind=kLoop, calls=%fused_computation.88 | loop fusion | flops 8902656 | bytes 5365760 | tf_op jit(solution)/shard_map/reduce_sum | solution.py:49
  34.5 0.8 slice.204
  35.3 1.3 %collective-permute-start.4 = (f32[3,2048]{1,0:T(4,128)S(1)}, f32[3,2048]{1,0:T(4,128)S(1)}, u32[]{:S(2)}, u32[]{:S(2)}) collective-permute-start(f32[3,2048]{1,0:T(4,128)S(1)} %slice.204), channel_id=1, source_target_pairs={{4,0},{8,4},{12,8},{16,12},{20,16},{24,20},{28,24},{5,1},{9,5},{13... | collective-permute-start | bytes 73736 | tf_op jit(solution)/shard_map/ppermute | solution.py:10
  36.6 0.0 copy-start
  36.6 1.3 %fusion.34 = f32[128,2048]{1,0:T(8,128)} fusion(f32[128,2048]{1,0:T(8,128)S(1)} %get-tuple-element.36), kind=kLoop, calls=%fused_computation.78 | loop fusion | flops 1048576 | bytes 2097152 | tf_op jit(solution)/shard_map/mul | solution.py:29
  37.8 0.1 stack.85
  37.9 0.1 stack.78
  38.0 4.3 %collective-permute-done.4 = f32[3,2048]{1,0:T(4,128)S(1)} collective-permute-done((f32[3,2048]{1,0:T(4,128)S(1)}, f32[3,2048]{1,0:T(4,128)S(1)}, u32[]{:S(2)}, u32[]{:S(2)}) %collective-permute-start.4) | collective-permute-done | bytes 24608 | tf_op jit(solution)/shard_map/ppermute | solution.py:10
  42.3 3.8 %multiply_reduce_fusion.9 = (f32[2048]{0:T(1024)S(1)}, f32[2048]{0:T(1024)S(1)}, f32[2048]{0:T(1024)S(1)}, f32[2048]{0:T(1024)S(1)}, f32[2048]{0:T(1024)S(1)}, /*index=5*/f32[128,2048]{1,0:T(8,128)S(1)}) fusion(f32[128,2048]{1,0:T(8,128)S(1)} %copy-done, f32[3,2048]{1,0:T(4,128)S(1)} %collective-permute-done, f32[128,2048]{1,0:T(8,128)S(1)} %get-tuple-element.40, ...), kind=kLoop, calls=%fused_computation.73 | loop fusion | flops 7854080 | bytes 4317184 | tf_op jit(solution)/shard_map/reduce_sum | solution.py:46
  46.1 1.3 %collective-permute-start.5 = (f32[3,2048]{1,0:T(4,128)S(1)}, f32[3,2048]{1,0:T(4,128)S(1)}, u32[]{:S(2)}, u32[]{:S(2)}) collective-permute-start(f32[3,2048]{1,0:T(4,128)S(1)} %slice.209), channel_id=1, source_target_pairs={{4,0},{8,4},{12,8},{16,12},{20,16},{24,20},{28,24},{5,1},{9,5},{13... | collective-permute-start | bytes 73736 | tf_op jit(solution)/shard_map/ppermute | solution.py:10
  47.4 0.1 stack.71
  47.5 40.1 %all-gather = f32[24,5,2048]{2,1,0:T(8,128)S(1)} all-gather(f32[3,5,2048]{2,1,0:T(8,128)S(1)} %pad_maximum_fusion.6), channel_id=2, replica_groups=mesh['seq'=8,'chan'=4] {'seq'}, dimensions={0}, use_global_device_ids=true | all-gather | bytes 1105920 | tf_op jit(solution)/shard_map/all_gather | solution.py:51
  87.6 0.1 reduce_sum.159
  87.8 0.7 slice.214
  88.4 0.6 copy.12
  89.1 0.0 collective-permute-done.5
  89.1 1.4 %fusion.4 = f32[128,2048]{1,0:T(8,128)} fusion(f32[128,2048]{1,0:T(8,128)S(1)} %get-tuple-element.33, f32[3,2048]{1,0:T(4,128)S(1)} %collective-permute-done.5, f32[2048]{0:T(1024)S(1)} %bitcast.42, f32[2048]{0:T(1024)S(1)} %bitcast.44, f32[2048]{0:T(1024)S(1)} %bitcast.46, f32[2048]{0:T(1024)S(1)} %bitcast.48), kind=kLoop, calls=%fused_computation.28 | loop fusion | flops 2621440 | bytes 2154496 | tf_op jit(solution)/shard_map/add | solution.py:38
  (8 shorter events, 0.1 us)
Async XLA Ops:
  1.5 7.0 %collective-permute-start = (f32[3,2048]{1,0:T(4,128)S(1)}, f32[3,2048]{1,0:T(4,128)S(1)}, u32[]{:S(2)}, u32[]{:S(2)}) collective-permute-start(f32[3,2048]{1,0:T(4,128)S(1)} %slice.150), channel_id=1, source_target_pairs={{0,4},{4,8},{8,12},{12,16},{16,20},{20,24},{24,28},{1,5},{5,9},{9,... | collective-permute-start | bytes 73736 | tf_op jit(solution)/shard_map/ppermute | solution.py:10
  11.6 5.3 %collective-permute-start.1 = (f32[3,2048]{1,0:T(4,128)S(1)}, f32[3,2048]{1,0:T(4,128)S(1)}, u32[]{:S(2)}, u32[]{:S(2)}) collective-permute-start(f32[3,2048]{1,0:T(4,128)S(1)} %slice.189), channel_id=1, source_target_pairs={{0,4},{4,8},{8,12},{12,16},{16,20},{20,24},{24,28},{1,5},{5,9},{9,... | collective-permute-start | bytes 73736 | tf_op jit(solution)/shard_map/ppermute | solution.py:10
  16.9 6.6 %copy-start.1 = (f32[128,2048]{1,0:T(8,128)S(1)}, f32[128,2048]{1,0:T(8,128)}, u32[]{:S(2)}) copy-start(f32[128,2048]{1,0:T(8,128)} %param.7) | copy-start | bytes 3145732
  17.6 5.9 %collective-permute-start.2 = (f32[3,2048]{1,0:T(4,128)S(1)}, f32[3,2048]{1,0:T(4,128)S(1)}, u32[]{:S(2)}, u32[]{:S(2)}) collective-permute-start(f32[3,2048]{1,0:T(4,128)S(1)} %slice.194), channel_id=1, source_target_pairs={{0,4},{4,8},{8,12},{12,16},{16,20},{20,24},{24,28},{1,5},{5,9},{9,... | collective-permute-start | bytes 73736 | tf_op jit(solution)/shard_map/ppermute | solution.py:10
  25.0 7.0 %collective-permute-start.3 = (f32[3,2048]{1,0:T(4,128)S(1)}, f32[3,2048]{1,0:T(4,128)S(1)}, u32[]{:S(2)}, u32[]{:S(2)}) collective-permute-start(f32[3,2048]{1,0:T(4,128)S(1)} %slice.199), channel_id=1, source_target_pairs={{4,0},{8,4},{12,8},{16,12},{20,16},{24,20},{28,24},{5,1},{9,5},{13... | collective-permute-start | bytes 73736 | tf_op jit(solution)/shard_map/ppermute | solution.py:10
  35.3 7.0 %collective-permute-start.4 = (f32[3,2048]{1,0:T(4,128)S(1)}, f32[3,2048]{1,0:T(4,128)S(1)}, u32[]{:S(2)}, u32[]{:S(2)}) collective-permute-start(f32[3,2048]{1,0:T(4,128)S(1)} %slice.204), channel_id=1, source_target_pairs={{4,0},{8,4},{12,8},{16,12},{20,16},{24,20},{28,24},{5,1},{9,5},{13... | collective-permute-start | bytes 73736 | tf_op jit(solution)/shard_map/ppermute | solution.py:10
  36.6 5.7 %copy-start = (f32[128,2048]{1,0:T(8,128)S(1)}, f32[128,2048]{1,0:T(8,128)}, u32[]{:S(2)}) copy-start(f32[128,2048]{1,0:T(8,128)} %param.4) | copy-start | bytes 3145732
  46.1 43.0 %collective-permute-start.5 = (f32[3,2048]{1,0:T(4,128)S(1)}, f32[3,2048]{1,0:T(4,128)S(1)}, u32[]{:S(2)}, u32[]{:S(2)}) collective-permute-start(f32[3,2048]{1,0:T(4,128)S(1)} %slice.209), channel_id=1, source_target_pairs={{4,0},{8,4},{12,8},{16,12},{20,16},{24,20},{28,24},{5,1},{9,5},{13... | collective-permute-start | bytes 73736 | tf_op jit(solution)/shard_map/ppermute | solution.py:10
